TPU v7x, 32 devices: a whole 2x2x4 slice. The times are simulated.
32 devices in a mesh: groups: 2 (over x), seq: 16 (over z, y, core).
Axes of the slice: x: 2, y: 2, z: 4, core: 2. Of those that a mesh axis runs over, the one named last changes fastest.
Arguments:
- attn_query: bfloat16 [8192, 2048], P(('groups', 'seq')), parts along dimension 0, may hold values from -16 to 16
- attn_key: bfloat16 [8192, 2048], P(('groups', 'seq')), parts along dimension 0, may hold values from -16 to 16
- attn_value: bfloat16 [8192, 2048], P(('groups', 'seq')), parts along dimension 0, may hold values from -6 to 6
- mesa_query: bfloat16 [8192, 2048], P(('groups', 'seq')), parts along dimension 0, may hold values from -6 to 6
- mesa_key: bfloat16 [8192, 2048], P(('groups', 'seq')), parts along dimension 0, may hold values from -16 to 16
- log_decay: float32 [8192, 16], P(('groups', 'seq')), parts along dimension 0, may hold values from -1 to 0
- input_gate: float32 [8192, 16], P(('groups', 'seq')), parts along dimension 0, may hold values from 0.2 to 1
- regularizer: float32 [16, 128], replicated, may hold values from 0.5 to 4
Outputs:
- attention: bfloat16 [8192, 2048], P(('groups', 'seq')), parts along dimension 0
- mesa_out: bfloat16 [8192, 2048], P(('groups', 'seq')), parts along dimension 0
There are 2 independent parts, one for each index of `groups`. A program takes and returns all parts, laid end to end along the dimension named above; an argument that names none is the same for every part. Nothing has to cross between parts.
All inputs are finite; a program needn't handle non-finite values.
Results may differ from a plain program's by a relative error of at most 0.017.
Values may be sent and summed in bfloat16 or wider, within the bound.
A program may use at most 128 MiB of HBM per device.

v0:
```python
import jax
import jax.numpy as jnp
from jax import lax
from jax.sharding import PartitionSpec as P

WINDOW = 2048
SPAN = 64
CG_ITERS = 8


exact_mode = lax.Precision.HIGHEST
masked_score = -1e30


def prefix(shard, axis, join, neutral):
    place = lax.axis_index(axis)
    gathered = jax.tree.map(
        lambda a, kind: lax.all_gather(a.astype(kind), axis), shard, (jnp.bfloat16, jnp.bfloat16)
    )
    state = jax.tree.map(lambda a, e: jnp.zeros_like(a) + jnp.asarray(e, a.dtype), shard, neutral)

    def one(lap, state):
        return join(
            state,
            jax.tree.map(
                lambda a, own: lax.dynamic_index_in_dim(a, lap, 0, False).astype(own.dtype),
                gathered,
                shard,
            ),
        )

    return lax.fori_loop(0, place, one, state)


def passed_along(value, axis, steps):
    count = lax.axis_size(axis)
    first, last = (max(0, -steps), min(count, count - steps))
    return lax.ppermute(value, axis, [(source, source + steps) for source in range(first, last)])


def span_update(states, inputs, ridge_diag):
    gram_start, cross_start = states
    queries, key_rows, value_rows, log_rates, gate_rows = inputs
    q_heads = jnp.transpose(queries, (1, 0, 2))
    k_heads = jnp.transpose(key_rows, (1, 0, 2))
    v_heads = jnp.transpose(value_rows, (1, 0, 2))
    cumulative = jnp.transpose(jnp.cumsum(log_rates, axis=0))
    length = cumulative.shape[1]
    causal = (jnp.arange(length)[:, None] >= jnp.arange(length)[None, :])[None]
    distance = cumulative[:, :, None] - cumulative[:, None, :]
    decay_mix = (
        jnp.where(causal, jnp.exp(jnp.where(causal, distance, 0.0)), 0.0)
        * jnp.transpose(gate_rows)[:, None, :]
    )
    start_scale = jnp.exp(cumulative)[:, :, None]
    iterate = jnp.zeros_like(q_heads)
    remain = q_heads
    search = q_heads
    norm_now = jnp.sum(remain * remain, axis=-1, keepdims=True)
    for sweep_index in range(CG_ITERS):
        carried = start_scale * jnp.einsum("hcd,hed->hce", search, gram_start, precision=exact_mode)
        operator_products = jnp.einsum("hjd,hid->hji", search, k_heads, precision=exact_mode)
        local_part = jnp.einsum(
            "hji,hid->hjd", decay_mix * operator_products, k_heads, precision=exact_mode
        )
        image_vec = carried + local_part + ridge_diag[:, None, :] * search
        step_size = norm_now / (jnp.sum(search * image_vec, axis=-1, keepdims=True) + 1e-06)
        iterate = iterate + step_size * search
        remain = remain - step_size * image_vec
        norm_next = jnp.sum(remain * remain, axis=-1, keepdims=True)
        search = remain + norm_next / (norm_now + 1e-06) * search
        norm_now = norm_next
    products = jnp.einsum("hjd,hid->hji", iterate, k_heads, precision=exact_mode)
    mesa_rows = start_scale * jnp.einsum("hje,hde->hjd", iterate, cross_start, precision=exact_mode)
    mesa_rows = mesa_rows + jnp.einsum(
        "hji,hid->hjd", decay_mix * products, v_heads, precision=exact_mode
    )
    tail_weight = (jnp.exp(cumulative[:, -1:] - cumulative) * jnp.transpose(gate_rows))[:, :, None]
    end_scale = jnp.exp(cumulative[:, -1])[:, None, None]
    gram_end = end_scale * gram_start + jnp.einsum(
        "hid,hie->hde", k_heads * tail_weight, k_heads, precision=exact_mode
    )
    cross_end = end_scale * cross_start + jnp.einsum(
        "hid,hie->hde", v_heads * tail_weight, k_heads, precision=exact_mode
    )
    return ((gram_end, cross_end), jnp.transpose(mesa_rows, (1, 0, 2)))


def mesa_pass(
    queries, key_rows, value_rows, log_rates, gate_rows, ridge_diag, gram_start, cross_start
):
    row_total = queries.shape[0]
    span_count = row_total // SPAN

    def shaped(array_in):
        return array_in.reshape((span_count, SPAN) + array_in.shape[1:])

    def advance(states, inputs):
        return span_update(states, inputs, ridge_diag)

    finished, outputs = lax.scan(
        advance,
        (gram_start, cross_start),
        (
            shaped(queries),
            shaped(key_rows),
            shaped(value_rows),
            shaped(log_rates),
            shaped(gate_rows),
        ),
    )
    return outputs.reshape(row_total, -1)


def fold_block(state_now, queries, key_value, query_first, key_first):
    running_max, running_sum, weighted = state_now
    row_count, head_count, head_size = queries.shape
    key_rows = key_value[0].reshape(-1, head_count, head_size)
    value_rows = key_value[1].reshape(-1, head_count, head_size)
    scores = jnp.einsum(
        "qhd,khd->hqk", queries, key_rows, preferred_element_type=jnp.float32
    ) * head_size ** (-0.5)
    query_pos = query_first + jnp.arange(row_count, dtype=jnp.int32)[:, None]
    key_pos = key_first + jnp.arange(key_rows.shape[0], dtype=jnp.int32)[None, :]
    distance = query_pos - key_pos
    inside = ((distance >= 0) & (distance < WINDOW) & (key_pos >= 0))[None]
    scores = jnp.where(inside, scores, masked_score)
    new_max = jnp.maximum(running_max, jnp.max(scores, axis=-1))
    weights = jnp.exp(scores - new_max[:, :, None]) * inside.astype(jnp.float32)
    rescale = jnp.exp(running_max - new_max)
    running_sum = running_sum * rescale + jnp.sum(weights, axis=-1)
    weighted = weighted * rescale[:, :, None] + jnp.einsum(
        "hqk,khd->hqd", weights.astype(jnp.bfloat16), value_rows, preferred_element_type=jnp.float32
    )
    return (new_max, running_sum, weighted)


def combine_pair(earlier, later):
    return (earlier[0] + later[0], jnp.exp(later[0])[:, None, None] * earlier[1] + later[1])


def body(
    attn_query, attn_key, attn_value, mesa_query, mesa_key, log_decay, input_gate, regularizer
):
    row_count = attn_query.shape[0]
    head_count, head_size = regularizer.shape
    shape3 = (row_count, head_count, head_size)
    slab_first = lax.axis_index("seq") * row_count
    keys_float = mesa_key.astype(jnp.float32).reshape(shape3)
    slab_log = jnp.sum(log_decay, axis=0)
    tail_log = slab_log[None, :] - jnp.cumsum(log_decay, axis=0)
    weight_rows = (jnp.exp(tail_log) * input_gate)[:, :, None]
    gram_local = jnp.einsum(
        "lhd,lhe->hde", keys_float * weight_rows, keys_float, precision=exact_mode
    )
    zero_log = jnp.zeros_like(slab_log)
    zero_state = jnp.zeros_like(gram_local)
    gram_prefix = prefix((slab_log, gram_local), "seq", combine_pair, (zero_log, zero_state))[1]
    queries = attn_query.reshape(shape3)
    key_value = jnp.stack([attn_key, attn_value])
    state_now = (
        jnp.full((head_count, row_count), masked_score, jnp.float32),
        jnp.zeros((head_count, row_count), jnp.float32),
        jnp.zeros((head_count, row_count, head_size), jnp.float32),
    )
    state_now = fold_block(state_now, queries, key_value, slab_first, slab_first)
    reach = -(-WINDOW // row_count)
    moving = key_value
    for hop_index in range(1, reach + 1):
        moving = passed_along(moving, "seq", 1)
        state_now = fold_block(
            state_now, queries, moving, slab_first, slab_first - hop_index * row_count
        )
    normed = state_now[2] / state_now[1][:, :, None]
    attention = jnp.transpose(normed, (1, 0, 2)).reshape(row_count, -1).astype(jnp.bfloat16)
    values_float = attention.astype(jnp.float32).reshape(shape3)
    cross_local = jnp.einsum(
        "lhd,lhe->hde", values_float * weight_rows, keys_float, precision=exact_mode
    )
    cross_prefix = prefix((slab_log, cross_local), "seq", combine_pair, (zero_log, zero_state))[1]
    mesa_out = mesa_pass(
        mesa_query.astype(jnp.float32).reshape(shape3),
        keys_float,
        values_float,
        log_decay,
        input_gate,
        regularizer,
        gram_prefix,
        cross_prefix,
    )
    return (attention, mesa_out.astype(jnp.bfloat16))


def solution(mesh):
    return jax.shard_map(
        body,
        mesh=mesh,
        in_specs=(
            P(("groups", "seq"), None),
            P(("groups", "seq"), None),
            P(("groups", "seq"), None),
            P(("groups", "seq"), None),
            P(("groups", "seq"), None),
            P(("groups", "seq"), None),
            P(("groups", "seq"), None),
            P(),
        ),
        out_specs=(P(("groups", "seq"), None), P(("groups", "seq"), None)),
        check_vma=False,
    )
```

profile of v0, /device:TPU:29, one launch (start us, length us, event | category | flops | bytes accessed | tf_op | source)
XLA Modules:
  0.0 676.4 jit_solution(13662638637842191389)
XLA Ops:
  13.9 4.9 collective-permute-done
  21.4 26.1 %collective-permute-done.1 = bf16[2,256,2048]{1,2,0:T(8,128)(2,1)S(1)} collective-permute-done((bf16[2,256,2048]{1,2,0:T(8,128)(2,1)S(1)}, bf16[2,256,2048]{1,2,0:T(8,128)(2,1)S(1)}, u32[]{:S(2)}, u32[]{:S(2)}) %collective-permute-start.1) | collective-permute-done | bytes 2097184 | tf_op jit(solution)/shard_map/ppermute | solution.py:38
  50.1 26.2 %collective-permute-done.2 = bf16[2,256,2048]{1,2,0:T(8,128)(2,1)} collective-permute-done((bf16[2,256,2048]{1,2,0:T(8,128)(2,1)S(1)}, bf16[2,256,2048]{1,2,0:T(8,128)(2,1)}, u32[]{:S(2)}, u32[]{:S(2)}) %collective-permute-start.2) | collective-permute-done | bytes 2097184 | tf_op jit(solution)/shard_map/ppermute | solution.py:38
  83.6 5.0 fusion.161
  88.7 15.2 %collective-permute-done.3 = bf16[2,256,2048]{1,2,0:T(8,128)(2,1)} collective-permute-done((bf16[2,256,2048]{1,2,0:T(8,128)(2,1)}, bf16[2,256,2048]{1,2,0:T(8,128)(2,1)}, u32[]{:S(2)}, u32[]{:S(2)}) %collective-permute-start.3) | collective-permute-done | bytes 2097184 | tf_op jit(solution)/shard_map/ppermute | solution.py:38
  108.2 24.6 %collective-permute-done.4 = bf16[2,256,2048]{1,2,0:T(8,128)(2,1)} collective-permute-done((bf16[2,256,2048]{1,2,0:T(8,128)(2,1)}, bf16[2,256,2048]{1,2,0:T(8,128)(2,1)}, u32[]{:S(2)}, u32[]{:S(2)}) %collective-permute-start.4) | collective-permute-done | bytes 2097184 | tf_op jit(solution)/shard_map/ppermute | solution.py:38
  141.7 20.7 %collective-permute-done.5 = bf16[2,256,2048]{1,2,0:T(8,128)(2,1)S(1)} collective-permute-done((bf16[2,256,2048]{1,2,0:T(8,128)(2,1)}, bf16[2,256,2048]{1,2,0:T(8,128)(2,1)S(1)}, u32[]{:S(2)}, u32[]{:S(2)}) %collective-permute-start.5) | collective-permute-done | bytes 2097184 | tf_op jit(solution)/shard_map/ppermute | solution.py:38
  174.4 30.7 %collective-permute-done.6 = bf16[2,256,2048]{1,2,0:T(8,128)(2,1)S(1)} collective-permute-done((bf16[2,256,2048]{1,2,0:T(8,128)(2,1)S(1)}, bf16[2,256,2048]{1,2,0:T(8,128)(2,1)S(1)}, u32[]{:S(2)}, u32[]{:S(2)}) %collective-permute-start.6) | collective-permute-done | bytes 2097184 | tf_op jit(solution)/shard_map/ppermute | solution.py:38
  211.7 29.0 %collective-permute-done.7 = bf16[2,256,2048]{1,2,0:T(8,128)(2,1)S(1)} collective-permute-done((bf16[2,256,2048]{1,2,0:T(8,128)(2,1)S(1)}, bf16[2,256,2048]{1,2,0:T(8,128)(2,1)S(1)}, u32[]{:S(2)}, u32[]{:S(2)}) %collective-permute-start.7) | collective-permute-done | bytes 2097184 | tf_op jit(solution)/shard_map/ppermute | solution.py:38
  257.8 4.3 fusion.96
  273.5 7.3 %fusion.104 = bf16[256,16,128]{2,0,1:T(8,128)(2,1)S(1)} fusion(f32[16,256,128]{2,1,0:T(8,128)S(1)} %fusion.86, f32[16,256,128]{2,1,0:T(8,128)S(1)} %fusion.88, f32[16,256,128]{2,1,0:T(8,128)S(1)} %fusion.90, f32[16,256,128]{2,1,0:T(8,128)S(1)} %fusion.92, f32[16,256,128]{2,1,0:T(8,128)S(1)} %fusion.94, f32[16,256,128]{2,1,0:T(8,128)S(1)} %copy-done.95, ...), kind=kOutput, calls=%fused_computation.196 | convolution fusion | flops 283639808 | bytes 23576576 | tf_op jit(solution)/shard_map/hqk,khd->hqd/dot_general | solution.py:132
  289.4 68.2 %all-reduce = bf16[256]{0:T(256)(128)(2,1)S(1)} all-reduce(bf16[256]{0:T(256)(128)(2,1)S(1)} %dynamic-update-slice), channel_id=2, replica_groups=mesh['groups'=2,'seq'=16] {'seq'}, use_global_device_ids=true, to_apply=%add | all-reduce | flops 256 | bytes 1024
  363.3 20.3 %while.38 = (s32[]{:T(128)}, f32[16,128,128]{2,1,0:T(8,128)S(1)}, s32[]{:T(128)}, bf16[16,16]{1,0:T(8,128)(2,1)S(1)}, bf16[16,16,128,128]{3,2,1,0:T(8,128)(2,1)}, /*index=5*/s32[]{:T(128)}, s32[]{:T(128)}, s32[]{:T(128)}) while((s32[]{:T(128)}, f32[16,128,128]{2,1,0:T(8,128)S(1)}, s32[]{:T(128)}, bf16[16,16]{1,0:T(8,128)(2,1)S(1)}, ...), condition=%wide.region_22.23_spmd, body=%wide.region_21.22_spmd.sunk | while | flops 786453 | bytes 2621727 | solution.py:32
  390.9 13.0 %all-gather.8.cloned.1.call-done = bf16[256,128,128]{2,1,0:T(8,128)(2,1)} async-done(((bf16[16,128,128]{2,1,0:T(8,128)(2,1)}), bf16[256,128,128]{2,1,0:T(8,128)(2,1)}) %all-gather.8.cloned.1.call-update) | async-done | bytes 8388624 | tf_op jit(solution)/shard_map/all_gather | solution.py:18
  405.0 37.7 %while.39 = (s32[]{:T(128)}, f32[16,128,128]{2,1,0:T(8,128)}, s32[]{:T(128)}, bf16[16,16]{1,0:T(8,128)(2,1)S(1)}, bf16[16,16,128,128]{3,2,1,0:T(8,128)(2,1)}, /*index=5*/s32[]{:T(128)}, s32[]{:T(128)}, s32[]{:T(128)}) while((s32[]{:T(128)}, f32[16,128,128]{2,1,0:T(8,128)}, s32[]{:T(128)}, bf16[16,16]{1,0:T(8,128)(2,1)S(1)}, ...), condition=%wide.region_24.25_spmd, body=%wide.region_23.24_spmd.sunk | while | flops 786453 | bytes 2621727 | solution.py:32
  442.7 223.3 %while.40 = (s32[]{:T(128)}, f32[16,128,128]{2,1,0:T(8,128)S(1)}, f32[16,128,128]{2,1,0:T(8,128)}, bf16[4,64,16,128]{3,1,2,0:T(8,128)(2,1)}, f32[4,64,16]{2,1,0:...) while((s32[]{:T(128)}, f32[16,128,128]{2,1,0:T(8,128)S(1)}, ...), condition=%wide.region_43.44_spmd, body=%wide.region_25.43_spmd.sunk | while | flops 4045949952 | bytes 85774864 | solution.py:101
  487.1 4.4 fusion.472
  493.6 4.4 convolution_add_fusion.5
  542.5 4.4 fusion.472
  549.0 4.4 convolution_add_fusion.5
  598.0 4.4 fusion.472
  604.5 4.4 convolution_add_fusion.5
  653.3 4.4 fusion.472
  659.9 4.4 convolution_add_fusion.5
  (627 shorter events, 344.4 us)
Async XLA Ops:
  7.2 126.9 %copy-start = (bf16[256,2048]{1,0:T(8,128)(2,1)S(1)}, bf16[256,2048]{1,0:T(8,128)(2,1)}, u32[]{:S(2)}) copy-start(bf16[256,2048]{1,0:T(8,128)(2,1)} %param.14) | copy-start | bytes 3145732
  7.2 70.4 %copy-start.56 = (f32[256,16]{0,1:T(8,128)S(1)}, f32[256,16]{0,1:T(8,128)}, u32[]{:S(2)}) copy-start(f32[256,16]{0,1:T(8,128)} %param.19) | copy-start | bytes 49156
  7.2 71.3 %copy-start.4 = (bf16[256,2048]{1,0:T(8,128)(2,1)S(1)}, bf16[256,2048]{1,0:T(8,128)(2,1)}, u32[]{:S(2)}) copy-start(bf16[256,2048]{1,0:T(8,128)(2,1)} %param.18) | copy-start | bytes 3145732
  7.2 355.9 %all-gather.6.cloned.1.call-start = ((), (), s32[]{:S(2)}) async-start(), calls=%async_computation | async-start | bytes 8912896 | tf_op jit(solution)/shard_map/all_gather | solution.py:18
  12.6 6.2 collective-permute-start
  20.1 27.3 %collective-permute-start.1 = (bf16[2,256,2048]{1,2,0:T(8,128)(2,1)S(1)}, bf16[2,256,2048]{1,2,0:T(8,128)(2,1)S(1)}, u32[]{:S(2)}, u32[]{:S(2)}) collective-permute-start(bf16[2,256,2048]{1,2,0:T(8,128)(2,1)S(1)} %collective-permute-done), channel_id=1, source_target_pairs={{0,1},{1,2},{2,3},{3,4},{4,5},{5,6},{6,7},{7,8},{8,9},{9,10},{10,1... | collective-permute-start | bytes 6291464 | tf_op jit(solution)/shard_map/ppermute | solution.py:38
  48.8 27.5 %collective-permute-start.2 = (bf16[2,256,2048]{1,2,0:T(8,128)(2,1)S(1)}, bf16[2,256,2048]{1,2,0:T(8,128)(2,1)}, u32[]{:S(2)}, u32[]{:S(2)}) collective-permute-start(bf16[2,256,2048]{1,2,0:T(8,128)(2,1)S(1)} %collective-permute-done.1), channel_id=1, source_target_pairs={{0,1},{1,2},{2,3},{3,4},{4,5},{5,6},{6,7},{7,8},{8,9},{9,10},{10,1... | collective-permute-start | bytes 6291464 | tf_op jit(solution)/shard_map/ppermute | solution.py:38
  76.3 27.7 %collective-permute-start.3 = (bf16[2,256,2048]{1,2,0:T(8,128)(2,1)}, bf16[2,256,2048]{1,2,0:T(8,128)(2,1)}, u32[]{:S(2)}, u32[]{:S(2)}) collective-permute-start(bf16[2,256,2048]{1,2,0:T(8,128)(2,1)} %collective-permute-done.2), channel_id=1, source_target_pairs={{0,1},{1,2},{2,3},{3,4},{4,5},{5,6},{6,7},{7,8},{8,9},{9,10},{10,1... | collective-permute-start | bytes 6291464 | tf_op jit(solution)/shard_map/ppermute | solution.py:38
  83.6 52.6 %copy-start.60 = (f32[256,16]{0,1:T(8,128)}, f32[256,16]{0,1:T(8,128)S(1)}, u32[]{:S(2)}) copy-start(f32[256,16]{0,1:T(8,128)S(1)} %fusion.228) | copy-start | bytes 49156
  88.7 315.2 %all-gather.8.cloned.1.call-start = ((), (), s32[]{:S(2)}) async-start(), calls=%async_computation.1 | async-start | bytes 8912896 | tf_op jit(solution)/shard_map/all_gather | solution.py:18
  103.9 28.9 %collective-permute-start.4 = (bf16[2,256,2048]{1,2,0:T(8,128)(2,1)}, bf16[2,256,2048]{1,2,0:T(8,128)(2,1)}, u32[]{:S(2)}, u32[]{:S(2)}) collective-permute-start(bf16[2,256,2048]{1,2,0:T(8,128)(2,1)} %collective-permute-done.3), channel_id=1, source_target_pairs={{0,1},{1,2},{2,3},{3,4},{4,5},{5,6},{6,7},{7,8},{8,9},{9,10},{10,1... | collective-permute-start | bytes 6291464 | tf_op jit(solution)/shard_map/ppermute | solution.py:38
  105.5 30.8 %copy-start.9 = (bf16[2,256,2048]{1,2,0:T(8,128)(2,1)S(1)}, bf16[2,256,2048]{1,2,0:T(8,128)(2,1)}, u32[]{:S(2)}) copy-start(bf16[2,256,2048]{1,2,0:T(8,128)(2,1)} %copy-done.8) | copy-start | bytes 6291460
  108.1 32.7 %copy-start.49 = (pred[256,256]{0,1:T(8,128)(4,1)}, pred[256,256]{0,1:T(8,128)(4,1)S(1)}, u32[]{:S(2)}) copy-start(pred[256,256]{0,1:T(8,128)(4,1)S(1)} %get-tuple-element.327) | copy-start | bytes 196612
  108.1 58.3 %copy-start.46 = (pred[256,256]{0,1:T(8,128)(4,1)}, pred[256,256]{0,1:T(8,128)(4,1)S(1)}, u32[]{:S(2)}) copy-start(pred[256,256]{0,1:T(8,128)(4,1)S(1)} %get-tuple-element.329) | copy-start | bytes 196612
  108.1 62.0 %copy-start.43 = (pred[256,256]{0,1:T(8,128)(4,1)}, pred[256,256]{0,1:T(8,128)(4,1)S(1)}, u32[]{:S(2)}) copy-start(pred[256,256]{0,1:T(8,128)(4,1)S(1)} %get-tuple-element.331) | copy-start | bytes 196612
  108.1 98.4 %copy-start.40 = (pred[256,256]{0,1:T(8,128)(4,1)}, pred[256,256]{0,1:T(8,128)(4,1)S(1)}, u32[]{:S(2)}) copy-start(pred[256,256]{0,1:T(8,128)(4,1)S(1)} %get-tuple-element.333) | copy-start | bytes 196612
  108.1 100.5 %copy-start.37 = (pred[256,256]{0,1:T(8,128)(4,1)}, pred[256,256]{0,1:T(8,128)(4,1)S(1)}, u32[]{:S(2)}) copy-start(pred[256,256]{0,1:T(8,128)(4,1)S(1)} %get-tuple-element.335) | copy-start | bytes 196612
  132.8 29.7 %collective-permute-start.5 = (bf16[2,256,2048]{1,2,0:T(8,128)(2,1)}, bf16[2,256,2048]{1,2,0:T(8,128)(2,1)S(1)}, u32[]{:S(2)}, u32[]{:S(2)}) collective-permute-start(bf16[2,256,2048]{1,2,0:T(8,128)(2,1)} %collective-permute-done.4), channel_id=1, source_target_pairs={{0,1},{1,2},{2,3},{3,4},{4,5},{5,6},{6,7},{7,8},{8,9},{9,10},{10,1... | collective-permute-start | bytes 6291464 | tf_op jit(solution)/shard_map/ppermute | solution.py:38
  136.2 106.6 %copy-start.58 = (f32[16,256]{1,0:T(8,128)}, f32[16,256]{1,0:T(8,128)S(1)}, u32[]{:S(2)}) copy-start(f32[16,256]{1,0:T(8,128)S(1)} %get-tuple-element.357) | copy-start | bytes 49156
  136.3 107.7 %copy-start.6 = (f32[16,256,256]{1,2,0:T(8,128)}, f32[16,256,256]{1,2,0:T(8,128)S(1)}, u32[]{:S(2)}) copy-start(f32[16,256,256]{1,2,0:T(8,128)S(1)} %get-tuple-element.358) | copy-start | bytes 12582916
  162.5 42.6 %collective-permute-start.6 = (bf16[2,256,2048]{1,2,0:T(8,128)(2,1)S(1)}, bf16[2,256,2048]{1,2,0:T(8,128)(2,1)S(1)}, u32[]{:S(2)}, u32[]{:S(2)}) collective-permute-start(bf16[2,256,2048]{1,2,0:T(8,128)(2,1)S(1)} %collective-permute-done.5), channel_id=1, source_target_pairs={{0,1},{1,2},{2,3},{3,4},{4,5},{5,6},{6,7},{7,8},{8,9},{9,10},{10,1... | collective-permute-start | bytes 6291464 | tf_op jit(solution)/shard_map/ppermute | solution.py:38
  205.1 35.6 %collective-permute-start.7 = (bf16[2,256,2048]{1,2,0:T(8,128)(2,1)S(1)}, bf16[2,256,2048]{1,2,0:T(8,128)(2,1)S(1)}, u32[]{:S(2)}, u32[]{:S(2)}) collective-permute-start(bf16[2,256,2048]{1,2,0:T(8,128)(2,1)S(1)} %collective-permute-done.6), channel_id=1, source_target_pairs={{0,1},{1,2},{2,3},{3,4},{4,5},{5,6},{6,7},{7,8},{8,9},{9,10},{10,1... | collective-permute-start | bytes 6291464 | tf_op jit(solution)/shard_map/ppermute | solution.py:38
  287.6 73.6 %copy-start.12 = (bf16[256,2048]{1,0:T(8,128)(2,1)S(1)}, bf16[256,2048]{1,0:T(8,128)(2,1)}, u32[]{:S(2)}) copy-start(bf16[256,2048]{1,0:T(8,128)(2,1)} %param.17) | copy-start | bytes 3145732
  405.0 37.7 %copy-start.3 = (f32[16,128]{1,0:T(8,128)S(1)}, f32[16,128]{1,0:T(8,128)}, u32[]{:S(2)}) copy-start(f32[16,128]{1,0:T(8,128)} %param.21) | copy-start | bytes 24580
  (85 other events, 280.3 us)
Sparse Core Ops, SparseCore 0:
  88.8 113.5 all-gather.5
  284.5 119.3 all-gather.7
where the time goes:
time: 687 us; the launch traced here: 676 us
  matrix products  227 us (33%)
  waiting for transfers between devices  190 us (28%)
  other arithmetic  104 us (15%)
  blocking collectives  68.2 us (10%)
  local copies, waits for them, and re-layouts  54.8 us (8%)
  between operations  16.6 us (2%)
  starting transfers between devices  10.5 us (2%)
    ppermute x8, waiting for transfers between devices, passed_along(): lax.ppermute(value, axis, [(source, source + steps) for source in range(f...  177 us
    dot_general x32, matrix products, span_update(): jnp.einsum('hcd,hed->hce', search, gram_start, precision=exact_mode)  73.5 us
    unnamed x1, blocking collectives  68.2 us
    add x30, other arithmetic, combine_pair(): jnp.exp(later[0])[:, None, None] * earlier[1] + later[1]  57.1 us
    dot_general x32, matrix products, span_update(): jnp.einsum('hjd,hid->hji', search, k_heads, precision=exact_mode)  32.5 us
    dot_general x9, matrix products, fold_block(): jnp.einsum('hqk,khd->hqd', weights.astype(jnp.bfloat16), value_rows, pref...  24 us
    dot_general x32, matrix products, span_update(): jnp.einsum('hji,hid->hjd', decay_mix * operator_products, k_heads, precis...  20.8 us
    dot_general x4, matrix products, span_update(): jnp.einsum('hid,hie->hde', v_heads * tail_weight, k_heads, precision=exac...  17.6 us
  transfers between devices with their start and end apart: 10, of which 9 were waited for; matrix products, arithmetic and copies ran while one was open for 17% of the time, Pallas kernels for 0%

commit v1 on v0

--- a/solution.py
+++ b/solution.py
@@ -1,7 +1,11 @@
 import jax
 import jax.numpy as jnp
 from jax import lax
+from jax.experimental import pallas as pl
+from jax.experimental.pallas import tpu as pltpu
 from jax.sharding import PartitionSpec as P
+import functools
+import math
 
 WINDOW = 2048
 SPAN = 64
@@ -139,7 +143,7 @@
     return (earlier[0] + later[0], jnp.exp(later[0])[:, None, None] * earlier[1] + later[1])
 
 
-def body(
+def slab_body(
     attn_query, attn_key, attn_value, mesa_query, mesa_key, log_decay, input_gate, regularizer
 ):
     row_count = attn_query.shape[0]
@@ -191,20 +195,255 @@
     return (attention, mesa_out.astype(jnp.bfloat16))
 
 
+CHUNK = 128
+WAYS = 4
+BF16 = jnp.bfloat16
+F32 = jnp.float32
+NT = (((1,), (1,)), ((), ()))
+TN = (((0,), (0,)), ((), ()))
+
+
+def dot(a, b, dims=None):
+    if dims is None:
+        return jnp.dot(a, b, preferred_element_type=F32)
+    return lax.dot_general(a, b, dims, preferred_element_type=F32)
+
+
+def two_terms(a):
+    high = a.astype(BF16)
+    low = (a - high.astype(F32)).astype(BF16)
+    return jnp.concatenate([high, low], axis=1)
+
+
+def attend_block(q_ref, k_ref, v_ref, out_ref, i, first, count, rows, banded):
+    scale = math.log2(math.e) / math.sqrt(q_ref.shape[1])
+    queries = q_ref[pl.ds(pl.multiple_of(i * rows, rows), rows), :]
+    base = pl.multiple_of(first * rows, rows)
+    row = lax.broadcasted_iota(jnp.int32, (rows, rows), 0)
+    col = lax.broadcasted_iota(jnp.int32, (rows, rows), 1)
+    scores, top = [], None
+    for j in range(count):
+        s = dot(queries, k_ref[pl.ds(base + j * rows, rows), :], NT)
+        if banded and j == 0:
+            s = jnp.where(row - col + (count - 1) * rows < WINDOW, s, masked_score)
+        if j == count - 1 or (not banded and j == count - 2):
+            s = jnp.where(row - col + (i - first - j) * rows >= 0, s, masked_score)
+        scores.append(s)
+        top = s if top is None else jnp.maximum(top, s)
+    top = jnp.max(top, axis=1, keepdims=True)
+    total, weights = None, []
+    for s in scores:
+        w = jnp.exp2((s - top) * scale)
+        total = w if total is None else total + w
+        weights.append(w.astype(BF16))
+    total = jnp.sum(total, axis=1, keepdims=True)
+    summed = dot(
+        jnp.concatenate(weights, axis=1), v_ref[pl.ds(base, count * rows), :]
+    )
+    out_ref[pl.ds(pl.multiple_of(i * rows, rows), rows), :] = (summed / total).astype(BF16)
+
+
+def attend_all(q_ref, k_ref, v_ref, out_ref, rows):
+    blocks = q_ref.shape[0] // rows
+    reach = WINDOW // rows
+    early = min(reach, blocks)
+    for low in range(0, early, 2):
+        high = min(low + 2, early)
+
+        def one(i, carry, high=high):
+            attend_block(q_ref, k_ref, v_ref, out_ref, i, 0, high, rows, False)
+            return carry
+
+        lax.fori_loop(low, high, one, 0)
+    if blocks > reach:
+
+        def late(i, carry):
+            attend_block(
+                q_ref, k_ref, v_ref, out_ref, i, i - reach, reach + 1, rows, True
+            )
+            return carry
+
+        lax.fori_loop(reach, blocks, late, 0)
+
+
+def span(c):
+    return pl.ds(pl.multiple_of(c * CHUNK, CHUNK), CHUNK)
+
+
+def column_form(row):
+    return jnp.transpose(jnp.broadcast_to(row, (CHUNK, CHUNK)))
+
+
+def tail_keys(k_ref, cum_ref, gate_ref, c):
+    cum, gate = cum_ref[pl.ds(c, 1), :], gate_ref[pl.ds(c, 1), :]
+    weight = column_form(jnp.exp(cum[:, CHUNK - 1 :] - cum) * gate)
+    keys = k_ref[span(c), :]
+    return (keys.astype(F32) * weight).astype(BF16), jnp.exp(cum[:, CHUNK - 1 :])
+
+
+def mix_of(cum_ref, gate_ref, c):
+    cum, gate = cum_ref[pl.ds(c, 1), :], gate_ref[pl.ds(c, 1), :]
+    col = column_form(cum)
+    shape = (CHUNK, CHUNK)
+    causal = lax.broadcasted_iota(jnp.int32, shape, 0) >= lax.broadcasted_iota(
+        jnp.int32, shape, 1
+    )
+    mix = jnp.exp(jnp.where(causal, col - cum, masked_score)) * gate
+    return mix, jnp.exp(col)
+
+
+def gram_states(k_ref, other_ref, cum_ref, gate_ref, starts_ref):
+    chunks = cum_ref.shape[0]
+
+    def step(g, state):
+        for w in range(WAYS):
+            c = g * WAYS + w
+            starts_ref[c] = state.astype(BF16)
+            keys, end = tail_keys(k_ref, cum_ref, gate_ref, c)
+            state = end * state + dot(keys, other_ref[span(c), :], TN)
+        return state
+
+    lax.fori_loop(0, chunks // WAYS, step, jnp.zeros((CHUNK, CHUNK), F32))
+
+
+def solve_all(q_ref, k_ref, cum_ref, gate_ref, ridge_ref, gram_ref, x_ref):
+    ridge = ridge_ref[...]
+    chunks = cum_ref.shape[0]
+
+    def group(g, carry):
+        ids = [g * WAYS + w for w in range(WAYS)]
+        mixes = [mix_of(cum_ref, gate_ref, c) for c in ids]
+        keys = [k_ref[span(c), :] for c in ids]
+        grams = [gram_ref[c] for c in ids]
+        sides = [
+            jnp.concatenate(
+                [jnp.concatenate([a, a], axis=1), jnp.concatenate([k, k], axis=1)], axis=0
+            )
+            for a, k in zip(grams, keys)
+        ]
+        stacks = [jnp.concatenate([k, k], axis=0) for k in keys]
+        state = []
+        for c in ids:
+            q = q_ref[span(c), :].astype(F32)
+            state.append((jnp.zeros_like(q), q, q, jnp.sum(q * q, axis=1, keepdims=True)))
+
+        def sweep(n, state):
+            both = [dot(two_terms(s[2]), side, NT) for s, side in zip(state, sides)]
+            local = [
+                dot(two_terms(m[0] * b[:, CHUNK:]), k) for m, b, k in zip(mixes, both, stacks)
+            ]
+            out = []
+            for (x, r, p, rr), b, l, m in zip(state, both, local, mixes):
+                a = m[1] * b[:, :CHUNK] + l + ridge * p
+                alpha = rr / (jnp.sum(p * a, axis=1, keepdims=True) + 1e-6)
+                x = x + alpha * p
+                r = r - alpha * a
+                new = jnp.sum(r * r, axis=1, keepdims=True)
+                p = r + (new / (rr + 1e-6)) * p
+                out.append((x, r, p, new))
+            return tuple(out)
+
+        state = lax.fori_loop(0, CG_ITERS, sweep, tuple(state))
+        for c, s in zip(ids, state):
+            x_ref[span(c), :] = s[0]
+        return carry
+
+    lax.fori_loop(0, chunks // WAYS, group, 0)
+
+
+def read_out(k_ref, v_ref, cum_ref, gate_ref, cross_ref, x_ref, out_ref):
+    chunks = cum_ref.shape[0]
+
+    def group(g, carry):
+        for w in range(WAYS):
+            c = g * WAYS + w
+            mix, start = mix_of(cum_ref, gate_ref, c)
+            keys, values, cross = k_ref[span(c), :], v_ref[span(c), :], cross_ref[c]
+            x = two_terms(x_ref[span(c), :])
+            products = dot(x, jnp.concatenate([keys, keys], axis=1), NT)
+            rows = start * dot(x, jnp.concatenate([cross, cross], axis=0))
+            rows = rows + dot(
+                two_terms(mix * products), jnp.concatenate([values, values], axis=0)
+            )
+            out_ref[span(c), :] = rows.astype(BF16)
+        return carry
+
+    lax.fori_loop(0, chunks // WAYS, group, 0)
+
+
+def head_kernel(
+    rows, q, k, v, mq, mk, cum, gate, ridge, att, out, gram, cross, x
+):
+    attend_all(q, k, v, att, rows)
+    gram_states(mk, mk, cum, gate, gram)
+    solve_all(mq, mk, cum, gate, ridge, gram, x)
+    gram_states(mk, att, cum, gate, cross)
+    read_out(mk, att, cum, gate, cross, x, out)
+
+
+def head_body(
+    attn_query, attn_key, attn_value, mesa_query, mesa_key, log_decay, input_gate, regularizer
+):
+    rows = attn_query.shape[0]
+    heads, size = regularizer.shape
+    devices = lax.axis_size("seq")
+    tokens = rows * devices
+
+    def to_heads(a):
+        return lax.all_to_all(a, "seq", 1, 0, tiled=True)
+
+    q, k, v, mq, mk = (
+        to_heads(a) for a in (attn_query, attn_key, attn_value, mesa_query, mesa_key)
+    )
+    rates = jnp.stack([jnp.transpose(log_decay), jnp.transpose(input_gate)], axis=1)
+    rates = lax.all_to_all(rates, "seq", 0, 0, tiled=True)
+    chunks = tokens // CHUNK
+    cum = jnp.cumsum(rates[:, 0].reshape(chunks, CHUNK), axis=1)
+    gate = rates[:, 1].reshape(chunks, CHUNK)
+    ridge = lax.dynamic_slice_in_dim(regularizer, lax.axis_index("seq"), 1, 0)
+    whole = jax.ShapeDtypeStruct((tokens, size), BF16)
+    vmem = pl.BlockSpec(memory_space=pltpu.VMEM)
+    att, out = pl.pallas_call(
+        functools.partial(head_kernel, rows),
+        out_shape=(whole, whole),
+        in_specs=[vmem] * 8,
+        out_specs=(vmem, vmem),
+        scratch_shapes=[
+            pltpu.VMEM((chunks, size, size), BF16),
+            pltpu.VMEM((chunks, size, size), BF16),
+            pltpu.VMEM((tokens, size), F32),
+        ],
+        compiler_params=pltpu.CompilerParams(vmem_limit_bytes=56 * 1024 * 1024),
+    )(q, k, v, mq, mk, cum, gate, ridge)
+
+    def to_slabs(a):
+        return lax.all_to_all(a, "seq", 0, 1, tiled=True)
+
+    return to_slabs(att), to_slabs(out)
+
+
+def fits_heads(mesh, rows, heads, size):
+    tokens = rows * mesh.shape["seq"]
+    return (
+        mesh.shape["seq"] == heads
+        and size == CHUNK
+        and WINDOW % rows == 0
+        and tokens % (CHUNK * WAYS) == 0
+    )
+
+
 def solution(mesh):
+    spec = P(("groups", "seq"), None)
+
+    def body(*args):
+        heads, size = args[7].shape
+        chosen = head_body if fits_heads(mesh, args[0].shape[0], heads, size) else slab_body
+        return chosen(*args)
+
     return jax.shard_map(
         body,
         mesh=mesh,
-        in_specs=(
-            P(("groups", "seq"), None),
-            P(("groups", "seq"), None),
-            P(("groups", "seq"), None),
-            P(("groups", "seq"), None),
-            P(("groups", "seq"), None),
-            P(("groups", "seq"), None),
-            P(("groups", "seq"), None),
-            P(),
-        ),
-        out_specs=(P(("groups", "seq"), None), P(("groups", "seq"), None)),
+        in_specs=(spec,) * 7 + (P(),),
+        out_specs=(spec, spec),
         check_vma=False,
     )

time: 687 us -> 307 us (0.45); the launches traced: 676 us -> 305 us
  matrix products: 227 us -> 0 us
  other arithmetic: 104 us -> 1.54 us
  Pallas kernels: 0 us -> 79.7 us
  waiting for transfers between devices: 190 us -> 132 us
  blocking collectives: 68.2 us -> 29.7 us
  local copies, waits for them, and re-layouts: 54.8 us -> 17.9 us
  starting transfers between devices: 10.5 us -> 42.8 us
  between operations: 16.6 us -> 0.69 us
    dot_general x136 -> x0, matrix products: 227 us -> none  [the longest x32 73.5 us: span_update(): jnp.einsum('hcd,hed->hce', search, gram_start, precision=exact_mode)]
    ppermute x8 -> x0, waiting for transfers between devices: 177 us -> none  [passed_along(): lax.ppermute(value, axis, [(source, source + steps) for source in range(f...]
    all_to_all x0 -> x7, waiting for transfers between devices: none -> 132 us  [the longest x5 108 us: to_heads(): return lax.all_to_all(a, 'seq', 1, 0, tiled=True)]
    pallas_call x0 -> x1, Pallas kernels: none -> 79.7 us  [head_body(): pl.pallas_call(functools.partial(head_kernel, rows), out_shape=(whole, wh...]
    add x72 -> x0, other arithmetic: 70.8 us -> none  [the longest x30 57.1 us: combine_pair(): jnp.exp(later[0])[:, None, None] * earlier[1] + later[1]]
    unnamed x1 -> x0, blocking collectives: 68.2 us -> none
    all_to_all x0 -> x7, starting transfers between devices: none -> 42.8 us  [the longest x5 30.8 us: to_heads(): return lax.all_to_all(a, 'seq', 1, 0, tiled=True)]
    all_to_all x0 -> x1, blocking collectives: none -> 29.7 us  [to_slabs(): return lax.all_to_all(a, 'seq', 0, 1, tiled=True)]
  transfers between devices with their start and end apart: 10 -> 7, of which waited for: 9 -> 7; matrix products, arithmetic and copies ran while one was open for 17% -> 5% of each run, Pallas kernels for 0% -> 0%
where the time goes in v1:
time: 307 us; the launch traced here: 305 us
  waiting for transfers between devices  132 us (43%)
  Pallas kernels  79.7 us (26%)
  starting transfers between devices  42.8 us (14%)
  blocking collectives  29.7 us (10%)
  local copies, waits for them, and re-layouts  17.9 us (6%)
    all_to_all x5, waiting for transfers between devices, to_heads(): return lax.all_to_all(a, 'seq', 1, 0, tiled=True)  108 us
    pallas_call x1, Pallas kernels, head_body(): pl.pallas_call(functools.partial(head_kernel, rows), out_shape=(whole, wh...  79.7 us
    all_to_all x5, starting transfers between devices, to_heads(): return lax.all_to_all(a, 'seq', 1, 0, tiled=True)  30.8 us
    all_to_all x1, blocking collectives, to_slabs(): return lax.all_to_all(a, 'seq', 0, 1, tiled=True)  29.7 us
    all_to_all x1, waiting for transfers between devices, to_slabs(): return lax.all_to_all(a, 'seq', 0, 1, tiled=True)  22.8 us
    all_to_all x5, local copies, waits for them, and re-layouts, to_heads(): return lax.all_to_all(a, 'seq', 1, 0, tiled=True)  9.91 us
    all_to_all x1, starting transfers between devices, head_body(): rates = lax.all_to_all(rates, 'seq', 0, 0, tiled=True)  6.3 us
  transfers between devices with their start and end apart: 7, of which 7 were waited for; matrix products, arithmetic and copies ran while one was open for 5% of the time, Pallas kernels for 0%

profile of v1, /device:TPU:29, one launch (start us, length us, event | category | flops | bytes accessed | tf_op | source)
XLA Modules:
  0.0 304.6 jit_solution(5160108417439724246)
XLA Ops:
  2.2 6.3 %all-to-all-start.5 = ((f32[16,2,256]{2,1,0:T(2,128)}), f32[16,2,256]{2,1,0:T(2,128)S(1)}, u32[]{:S(2)}, u32[]{:S(2)}) async-start(f32[16,2,256]{2,1,0:T(2,128)} %pad_maximum_fusion), calls=%async_computation.5 | async-start | bytes 65536 | tf_op jit(solution)/shard_map/all_to_all | solution.py:399
  8.5 1.2 copy_bitcast_fusion.6
  9.7 1.2 all-to-all-done.5
  10.9 7.8 %all-to-all-start = ((bf16[256,16,128]{2,0,1:T(8,128)(2,1)}), bf16[256,16,128]{2,0,1:T(8,128)(2,1)S(1)}, u32[]{:S(2)}, u32[]{:S(2)}) async-start(bf16[256,16,128]{2,0,1:T(8,128)(2,1)} %copy_bitcast_fusion.6), calls=%async_computation | async-start | bytes 2097152 | tf_op jit(solution)/shard_map/all_to_all | solution.py:393
  18.7 1.2 copy_bitcast_fusion.5
  20.0 22.6 %all-to-all-done = bf16[256,16,128]{2,0,1:T(8,128)(2,1)S(1)} async-done(((bf16[256,16,128]{2,0,1:T(8,128)(2,1)}), bf16[256,16,128]{2,0,1:T(8,128)(2,1)S(1)}, u32[]{:S(2)}, u32[]{:S(2)}) %all-to-all-start) | async-done | bytes 1048608 | tf_op jit(solution)/shard_map/all_to_all | solution.py:393
  42.6 5.7 %all-to-all-start.1 = ((bf16[256,16,128]{2,0,1:T(8,128)(2,1)}), bf16[256,16,128]{2,0,1:T(8,128)(2,1)S(1)}, u32[]{:S(2)}, u32[]{:S(2)}) async-start(bf16[256,16,128]{2,0,1:T(8,128)(2,1)} %copy_bitcast_fusion.5), calls=%async_computation.1 | async-start | bytes 2097152 | tf_op jit(solution)/shard_map/all_to_all | solution.py:393
  48.4 2.5 copy_bitcast_fusion.4
  50.8 21.5 %all-to-all-done.1 = bf16[256,16,128]{2,0,1:T(8,128)(2,1)S(1)} async-done(((bf16[256,16,128]{2,0,1:T(8,128)(2,1)}), bf16[256,16,128]{2,0,1:T(8,128)(2,1)S(1)}, u32[]{:S(2)}, u32[]{:S(2)}) %all-to-all-start.1) | async-done | bytes 1048608 | tf_op jit(solution)/shard_map/all_to_all | solution.py:393
  72.3 5.7 %all-to-all-start.2 = ((bf16[256,16,128]{2,0,1:T(8,128)(2,1)}), bf16[256,16,128]{2,0,1:T(8,128)(2,1)S(1)}, u32[]{:S(2)}, u32[]{:S(2)}) async-start(bf16[256,16,128]{2,0,1:T(8,128)(2,1)} %copy_bitcast_fusion.4), calls=%async_computation.2 | async-start | bytes 2097152 | tf_op jit(solution)/shard_map/all_to_all | solution.py:393
  78.0 2.5 copy_bitcast_fusion.3
  80.5 21.5 %all-to-all-done.2 = bf16[256,16,128]{2,0,1:T(8,128)(2,1)S(1)} async-done(((bf16[256,16,128]{2,0,1:T(8,128)(2,1)}), bf16[256,16,128]{2,0,1:T(8,128)(2,1)S(1)}, u32[]{:S(2)}, u32[]{:S(2)}) %all-to-all-start.2) | async-done | bytes 1048608 | tf_op jit(solution)/shard_map/all_to_all | solution.py:393
  103.0 5.7 %all-to-all-start.3 = ((bf16[256,16,128]{2,0,1:T(8,128)(2,1)}), bf16[256,16,128]{2,0,1:T(8,128)(2,1)S(1)}, u32[]{:S(2)}, u32[]{:S(2)}) async-start(bf16[256,16,128]{2,0,1:T(8,128)(2,1)} %copy_bitcast_fusion.3), calls=%async_computation.3 | async-start | bytes 2097152 | tf_op jit(solution)/shard_map/all_to_all | solution.py:393
  108.7 2.5 copy_bitcast_fusion.2
  111.2 21.5 %all-to-all-done.3 = bf16[256,16,128]{2,0,1:T(8,128)(2,1)S(1)} async-done(((bf16[256,16,128]{2,0,1:T(8,128)(2,1)}), bf16[256,16,128]{2,0,1:T(8,128)(2,1)S(1)}, u32[]{:S(2)}, u32[]{:S(2)}) %all-to-all-start.3) | async-done | bytes 1048608 | tf_op jit(solution)/shard_map/all_to_all | solution.py:393
  133.6 5.7 %all-to-all-start.4 = ((bf16[256,16,128]{2,0,1:T(8,128)(2,1)}), bf16[256,16,128]{2,0,1:T(8,128)(2,1)S(1)}, u32[]{:S(2)}, u32[]{:S(2)}) async-start(bf16[256,16,128]{2,0,1:T(8,128)(2,1)} %copy_bitcast_fusion.2), calls=%async_computation.4 | async-start | bytes 2097152 | tf_op jit(solution)/shard_map/all_to_all | solution.py:393
  139.4 1.3 constant_dynamic-slice_fusion.ridge
  142.2 21.2 %all-to-all-done.4 = bf16[256,16,128]{2,0,1:T(8,128)(2,1)S(1)} async-done(((bf16[256,16,128]{2,0,1:T(8,128)(2,1)}), bf16[256,16,128]{2,0,1:T(8,128)(2,1)S(1)}, u32[]{:S(2)}, u32[]{:S(2)}) %all-to-all-start.4) | async-done | bytes 1048608 | tf_op jit(solution)/shard_map/all_to_all | solution.py:393
  164.3 79.7 %shard_map.95 = (bf16[4096,128]{1,0:T(8,128)(2,1)}, bf16[4096,128]{1,0:T(8,128)(2,1)}) custom-call(bf16[4096,128]{1,0:T(8,128)(2,1)} %bitcast.58, bf16[4096,128]{1,0:T(8,128)(2,1)} %bitcast.59, bf16[4096,128]{1,0:T(8,128)(2,1)} %bitcast.60, bf16[4096,128]{1,0:T(8,128)(2,1)} %bitcast.61, bf16[4096,128]{1,0:T(8,128)(2,1)} %bitcast.62, ...), custom_call_target="tpu_custom_call" | custom-call | tf_op jit(solution)/shard_map/pallas_call | solution.py:406
  244.0 29.7 %all_to_all.138 = bf16[16,256,128]{2,1,0:T(8,128)(2,1)S(1)} all-to-all(bf16[16,256,128]{2,1,0:T(8,128)(2,1)} %bitcast.64), channel_id=1, replica_groups=mesh['groups'=2,'seq'=16] {'seq'}, dimensions={0} | all-to-all | bytes 2097152 | tf_op jit(solution)/shard_map/all_to_all | solution.py:420
  273.8 5.7 %all-to-all-start.6 = ((bf16[16,256,128]{2,1,0:T(8,128)(2,1)}), bf16[16,256,128]{2,1,0:T(8,128)(2,1)S(1)}, u32[]{:S(2)}, u32[]{:S(2)}) async-start(bf16[16,256,128]{2,1,0:T(8,128)(2,1)} %bitcast.63), calls=%async_computation.6 | async-start | bytes 2097152 | tf_op jit(solution)/shard_map/all_to_all | solution.py:420
  279.5 1.1 copy_bitcast_fusion
  280.6 22.8 %all-to-all-done.6 = bf16[16,256,128]{2,1,0:T(8,128)(2,1)S(1)} async-done(((bf16[16,256,128]{2,1,0:T(8,128)(2,1)}), bf16[16,256,128]{2,1,0:T(8,128)(2,1)S(1)}, u32[]{:S(2)}, u32[]{:S(2)}) %all-to-all-start.6) | async-done | bytes 1048608 | tf_op jit(solution)/shard_map/all_to_all | solution.py:420
  303.4 1.1 copy_bitcast_fusion.1
  (21 shorter events, 6.0 us)
Async XLA Ops:
  0.6 7.8 %copy-start = (bf16[256,2048]{1,0:T(8,128)(2,1)S(1)}, bf16[256,2048]{1,0:T(8,128)(2,1)}, u32[]{:S(2)}) copy-start(bf16[256,2048]{1,0:T(8,128)(2,1)} %param.8) | copy-start | bytes 3145732
  0.6 0.8 copy-start.7
  2.2 8.8 %all-to-all-start.5 = ((f32[16,2,256]{2,1,0:T(2,128)}), f32[16,2,256]{2,1,0:T(2,128)S(1)}, u32[]{:S(2)}, u32[]{:S(2)}) async-start(f32[16,2,256]{2,1,0:T(2,128)} %pad_maximum_fusion), calls=%async_computation.5 | async-start | bytes 65536 | tf_op jit(solution)/shard_map/all_to_all | solution.py:399
  9.7 9.0 %copy-start.6 = (bf16[256,2048]{1,0:T(8,128)(2,1)S(1)}, bf16[256,2048]{1,0:T(8,128)(2,1)}, u32[]{:S(2)}) copy-start(bf16[256,2048]{1,0:T(8,128)(2,1)} %param.9) | copy-start | bytes 3145732
  10.9 31.7 %all-to-all-start = ((bf16[256,16,128]{2,0,1:T(8,128)(2,1)}), bf16[256,16,128]{2,0,1:T(8,128)(2,1)S(1)}, u32[]{:S(2)}, u32[]{:S(2)}) async-start(bf16[256,16,128]{2,0,1:T(8,128)(2,1)} %copy_bitcast_fusion.6), calls=%async_computation | async-start | bytes 2097152 | tf_op jit(solution)/shard_map/all_to_all | solution.py:393
  42.6 8.2 %copy-start.1 = (bf16[256,16,128]{2,0,1:T(8,128)(2,1)}, bf16[256,16,128]{2,0,1:T(8,128)(2,1)S(1)}, u32[]{:S(2)}) copy-start(bf16[256,16,128]{2,0,1:T(8,128)(2,1)S(1)} %all-to-all-done) | copy-start | bytes 3145732
  42.6 29.7 %all-to-all-start.1 = ((bf16[256,16,128]{2,0,1:T(8,128)(2,1)}), bf16[256,16,128]{2,0,1:T(8,128)(2,1)S(1)}, u32[]{:S(2)}, u32[]{:S(2)}) async-start(bf16[256,16,128]{2,0,1:T(8,128)(2,1)} %copy_bitcast_fusion.5), calls=%async_computation.1 | async-start | bytes 2097152 | tf_op jit(solution)/shard_map/all_to_all | solution.py:393
  72.3 8.2 %copy-start.2 = (bf16[256,16,128]{2,0,1:T(8,128)(2,1)}, bf16[256,16,128]{2,0,1:T(8,128)(2,1)S(1)}, u32[]{:S(2)}) copy-start(bf16[256,16,128]{2,0,1:T(8,128)(2,1)S(1)} %all-to-all-done.1) | copy-start | bytes 3145732
  72.3 29.7 %all-to-all-start.2 = ((bf16[256,16,128]{2,0,1:T(8,128)(2,1)}), bf16[256,16,128]{2,0,1:T(8,128)(2,1)S(1)}, u32[]{:S(2)}, u32[]{:S(2)}) async-start(bf16[256,16,128]{2,0,1:T(8,128)(2,1)} %copy_bitcast_fusion.4), calls=%async_computation.2 | async-start | bytes 2097152 | tf_op jit(solution)/shard_map/all_to_all | solution.py:393
  102.0 1.0 copy-start.3
  103.0 29.7 %all-to-all-start.3 = ((bf16[256,16,128]{2,0,1:T(8,128)(2,1)}), bf16[256,16,128]{2,0,1:T(8,128)(2,1)S(1)}, u32[]{:S(2)}, u32[]{:S(2)}) async-start(bf16[256,16,128]{2,0,1:T(8,128)(2,1)} %copy_bitcast_fusion.3), calls=%async_computation.3 | async-start | bytes 2097152 | tf_op jit(solution)/shard_map/all_to_all | solution.py:393
  132.7 1.0 copy-start.4
  133.6 29.7 %all-to-all-start.4 = ((bf16[256,16,128]{2,0,1:T(8,128)(2,1)}), bf16[256,16,128]{2,0,1:T(8,128)(2,1)S(1)}, u32[]{:S(2)}, u32[]{:S(2)}) async-start(bf16[256,16,128]{2,0,1:T(8,128)(2,1)} %copy_bitcast_fusion.2), calls=%async_computation.4 | async-start | bytes 2097152 | tf_op jit(solution)/shard_map/all_to_all | solution.py:393
  163.3 1.0 copy-start.5
  273.8 29.7 %all-to-all-start.6 = ((bf16[16,256,128]{2,1,0:T(8,128)(2,1)}), bf16[16,256,128]{2,1,0:T(8,128)(2,1)S(1)}, u32[]{:S(2)}, u32[]{:S(2)}) async-start(bf16[16,256,128]{2,1,0:T(8,128)(2,1)} %bitcast.63), calls=%async_computation.6 | async-start | bytes 2097152 | tf_op jit(solution)/shard_map/all_to_all | solution.py:420

commit v2 on v1

--- a/solution.py
+++ b/solution.py
@@ -243,7 +243,7 @@
     out_ref[pl.ds(pl.multiple_of(i * rows, rows), rows), :] = (summed / total).astype(BF16)
 
 
-def attend_all(q_ref, k_ref, v_ref, out_ref, rows):
+def attend_all(q_ref, k_ref, v_ref, out_ref, rows, done):
     blocks = q_ref.shape[0] // rows
     reach = WINDOW // rows
     early = min(reach, blocks)
@@ -252,6 +252,7 @@
 
         def one(i, carry, high=high):
             attend_block(q_ref, k_ref, v_ref, out_ref, i, 0, high, rows, False)
+            done(i)
             return carry
 
         lax.fori_loop(low, high, one, 0)
@@ -261,28 +262,44 @@
             attend_block(
                 q_ref, k_ref, v_ref, out_ref, i, i - reach, reach + 1, rows, True
             )
+            done(i)
             return carry
 
         lax.fori_loop(reach, blocks, late, 0)
 
 
-def span(c):
-    return pl.ds(pl.multiple_of(c * CHUNK, CHUNK), CHUNK)
+def flat(c, per):
+    return c[0] * per + c[1]
+
+
+def span(c, per):
+    return pl.ds(pl.multiple_of(flat(c, per) * CHUNK, CHUNK), CHUNK)
+
+
+def chunk_ids(g, per, ways=WAYS):
+    slabs = ways // per
+    return [(g * slabs + w // per, w % per) for w in range(ways)]
 
 
 def column_form(row):
     return jnp.transpose(jnp.broadcast_to(row, (CHUNK, CHUNK)))
 
 
-def tail_keys(k_ref, cum_ref, gate_ref, c):
-    cum, gate = cum_ref[pl.ds(c, 1), :], gate_ref[pl.ds(c, 1), :]
+def rates_of(rates_ref, c):
+    slab, place = c
+    per = rates_ref.shape[1] // 4
+    return rates_ref[slab, place : place + 1, :], rates_ref[slab, per + place : per + place + 1, :]
+
+
+def tail_keys(k_ref, rates_ref, c, per):
+    cum, gate = rates_of(rates_ref, c)
     weight = column_form(jnp.exp(cum[:, CHUNK - 1 :] - cum) * gate)
-    keys = k_ref[span(c), :]
+    keys = k_ref[span(c, per), :]
     return (keys.astype(F32) * weight).astype(BF16), jnp.exp(cum[:, CHUNK - 1 :])
 
 
-def mix_of(cum_ref, gate_ref, c):
-    cum, gate = cum_ref[pl.ds(c, 1), :], gate_ref[pl.ds(c, 1), :]
+def mix_of(rates_ref, c):
+    cum, gate = rates_of(rates_ref, c)
     col = column_form(cum)
     shape = (CHUNK, CHUNK)
     causal = lax.broadcasted_iota(jnp.int32, shape, 0) >= lax.broadcasted_iota(
@@ -292,29 +309,30 @@
     return mix, jnp.exp(col)
 
 
-def gram_states(k_ref, other_ref, cum_ref, gate_ref, starts_ref):
-    chunks = cum_ref.shape[0]
+def gram_states(k_ref, other_ref, rates_ref, starts_ref):
+    per = rates_ref.shape[1] // 4
+    chunks = rates_ref.shape[0] * per
 
     def step(g, state):
-        for w in range(WAYS):
-            c = g * WAYS + w
-            starts_ref[c] = state.astype(BF16)
-            keys, end = tail_keys(k_ref, cum_ref, gate_ref, c)
-            state = end * state + dot(keys, other_ref[span(c), :], TN)
+        for c in chunk_ids(g, per):
+            starts_ref[flat(c, per)] = state.astype(BF16)
+            keys, end = tail_keys(k_ref, rates_ref, c, per)
+            state = end * state + dot(keys, other_ref[span(c, per), :], TN)
         return state
 
     lax.fori_loop(0, chunks // WAYS, step, jnp.zeros((CHUNK, CHUNK), F32))
 
 
-def solve_all(q_ref, k_ref, cum_ref, gate_ref, ridge_ref, gram_ref, x_ref):
-    ridge = ridge_ref[...]
-    chunks = cum_ref.shape[0]
+def solve_all(q_ref, k_ref, rates_ref, ridge_ref, gram_ref, x_ref):
+    ridge = ridge_ref
+    per = rates_ref.shape[1] // 4
+    chunks = rates_ref.shape[0] * per
 
     def group(g, carry):
-        ids = [g * WAYS + w for w in range(WAYS)]
-        mixes = [mix_of(cum_ref, gate_ref, c) for c in ids]
-        keys = [k_ref[span(c), :] for c in ids]
-        grams = [gram_ref[c] for c in ids]
+        ids = chunk_ids(g, per)
+        mixes = [mix_of(rates_ref, c) for c in ids]
+        keys = [k_ref[span(c, per), :] for c in ids]
+        grams = [gram_ref[flat(c, per)] for c in ids]
         sides = [
             jnp.concatenate(
                 [jnp.concatenate([a, a], axis=1), jnp.concatenate([k, k], axis=1)], axis=0
@@ -324,7 +342,7 @@
         stacks = [jnp.concatenate([k, k], axis=0) for k in keys]
         state = []
         for c in ids:
-            q = q_ref[span(c), :].astype(F32)
+            q = q_ref[span(c, per), :].astype(F32)
             state.append((jnp.zeros_like(q), q, q, jnp.sum(q * q, axis=1, keepdims=True)))
 
         def sweep(n, state):
@@ -345,40 +363,120 @@
 
         state = lax.fori_loop(0, CG_ITERS, sweep, tuple(state))
         for c, s in zip(ids, state):
-            x_ref[span(c), :] = s[0]
+            x_ref[span(c, per), :] = s[0]
         return carry
 
     lax.fori_loop(0, chunks // WAYS, group, 0)
 
 
-def read_out(k_ref, v_ref, cum_ref, gate_ref, cross_ref, x_ref, out_ref):
-    chunks = cum_ref.shape[0]
-
-    def group(g, carry):
-        for w in range(WAYS):
-            c = g * WAYS + w
-            mix, start = mix_of(cum_ref, gate_ref, c)
-            keys, values, cross = k_ref[span(c), :], v_ref[span(c), :], cross_ref[c]
-            x = two_terms(x_ref[span(c), :])
-            products = dot(x, jnp.concatenate([keys, keys], axis=1), NT)
-            rows = start * dot(x, jnp.concatenate([cross, cross], axis=0))
-            rows = rows + dot(
-                two_terms(mix * products), jnp.concatenate([values, values], axis=0)
-            )
-            out_ref[span(c), :] = rows.astype(BF16)
+def read_out(k_ref, v_ref, rates_ref, cross_ref, x_ref, out_ref, slab):
+    per = rates_ref.shape[1] // 4
+    for c in chunk_ids(slab, per, per):
+        mix, start = mix_of(rates_ref, c)
+        keys, values, cross = k_ref[span(c, per), :], v_ref[span(c, per), :], cross_ref[flat(c, per)]
+        x = two_terms(x_ref[span(c, per), :])
+        products = dot(x, jnp.concatenate([keys, keys], axis=1), NT)
+        rows = start * dot(x, jnp.concatenate([cross, cross], axis=0))
+        rows = rows + dot(two_terms(mix * products), jnp.concatenate([values, values], axis=0))
+        out_ref[span(c, per), :] = rows.astype(BF16)
+
+
+def head_kernel(n, *refs):
+    ins, rates_in, ridge_in = refs[:5], refs[5], refs[6]
+    results = refs[7:9]
+    bufs, rates, homes = refs[9:14], refs[14], refs[15:17]
+    gram, cross, x = refs[17:20]
+    send, recv, own = refs[20:23]
+    q, k, v, mk, mq = bufs
+    att, out = homes
+    rows, size = ins[0].shape[0], ridge_in.shape[1]
+    group, me = lax.axis_index("groups"), lax.axis_index("seq")
+
+    def row_block(ref, s):
+        return ref.at[pl.ds(pl.multiple_of(s * rows, rows), rows), :]
+
+    def col_block(ref, h):
+        return ref.at[:, pl.ds(pl.multiple_of(h * size, size), size)]
+
+    def ends(a, source, target):
+        if a < 5:
+            return col_block(ins[a], target), row_block(bufs[a], source)
+        if a == 5:
+            return rates_in.at[target], rates.at[source]
+        return row_block(homes[a - 6], target), col_block(results[a - 6], source)
+
+    def remote(a, source, target, peer):
+        src, dst = ends(a, source, target)
+        return pltpu.make_async_remote_copy(
+            src_ref=src,
+            dst_ref=dst,
+            send_sem=send.at[a, target],
+            recv_sem=recv.at[a, source],
+            device_id=(group, peer),
+            device_id_type=pl.DeviceIdType.MESH,
+        )
+
+    def local(a):
+        src, dst = ends(a, me, me)
+        return pltpu.make_async_copy(src, dst, own.at[a])
+
+    def other(t):
+        return lax.rem(me + t, n)
+
+    def over_peers(act):
+        def one(t, carry):
+            act(other(t))
+            return carry
+
+        lax.fori_loop(1, n, one, 0)
+
+    def arrive(a):
+        over_peers(lambda peer: remote(a, peer, me, peer).wait_recv())
+        local(a).wait()
+
+    def give(a, slab):
+        @pl.when(slab != me)
+        def _():
+            remote(a, me, slab, slab).start()
+
+        @pl.when(slab == me)
+        def _():
+            local(a).start()
+
+    barrier = pltpu.get_barrier_semaphore()
+    over_peers(
+        lambda peer: pl.semaphore_signal(
+            barrier, inc=1, device_id=(group, peer), device_id_type=pl.DeviceIdType.MESH
+        )
+    )
+    pl.semaphore_wait(barrier, n - 1)
+    for a in SEND_ORDER:
+        over_peers(lambda peer: remote(a, me, peer, peer).start())
+        local(a).start()
+
+    for a in (0, 1, 2):
+        arrive(a)
+    attend_all(q, k, v, att, rows, lambda i: give(6, i))
+    for a in (5, 3, 4):
+        arrive(a)
+    gram_states(mk, mk, rates, gram)
+    gram_states(mk, att, rates, cross)
+    solve_all(mq, mk, rates, ridge_in[pl.ds(me, 1), :], gram, x)
+
+    def slab_out(t, carry):
+        slab = other(t + 1)
+        read_out(mk, att, rates, cross, x, out, slab)
+        give(7, slab)
         return carry
 
-    lax.fori_loop(0, chunks // WAYS, group, 0)
-
-
-def head_kernel(
-    rows, q, k, v, mq, mk, cum, gate, ridge, att, out, gram, cross, x
-):
-    attend_all(q, k, v, att, rows)
-    gram_states(mk, mk, cum, gate, gram)
-    solve_all(mq, mk, cum, gate, ridge, gram, x)
-    gram_states(mk, att, cum, gate, cross)
-    read_out(mk, att, cum, gate, cross, x, out)
+    lax.fori_loop(0, n, slab_out, 0)
+    for a in (6, 7):
+        arrive(a)
+    for a in range(8):
+        over_peers(lambda peer: remote(a, me, peer, peer).wait_send())
+
+
+SEND_ORDER = (0, 1, 2, 5, 3, 4)
 
 
 def head_body(
@@ -388,38 +486,32 @@
     heads, size = regularizer.shape
     devices = lax.axis_size("seq")
     tokens = rows * devices
-
-    def to_heads(a):
-        return lax.all_to_all(a, "seq", 1, 0, tiled=True)
-
-    q, k, v, mq, mk = (
-        to_heads(a) for a in (attn_query, attn_key, attn_value, mesa_query, mesa_key)
-    )
-    rates = jnp.stack([jnp.transpose(log_decay), jnp.transpose(input_gate)], axis=1)
-    rates = lax.all_to_all(rates, "seq", 0, 0, tiled=True)
-    chunks = tokens // CHUNK
-    cum = jnp.cumsum(rates[:, 0].reshape(chunks, CHUNK), axis=1)
-    gate = rates[:, 1].reshape(chunks, CHUNK)
-    ridge = lax.dynamic_slice_in_dim(regularizer, lax.axis_index("seq"), 1, 0)
-    whole = jax.ShapeDtypeStruct((tokens, size), BF16)
+    per, chunks = rows // CHUNK, tokens // CHUNK
+    cum = jnp.cumsum(log_decay.reshape(per, CHUNK, heads), axis=1)
+    rates = jnp.concatenate([cum, input_gate.reshape(per, CHUNK, heads)], axis=0)
+    rates = jnp.pad(jnp.transpose(rates, (2, 0, 1)), ((0, 0), (0, 2 * per), (0, 0)))
+    slab = jax.ShapeDtypeStruct((rows, heads * size), BF16)
     vmem = pl.BlockSpec(memory_space=pltpu.VMEM)
-    att, out = pl.pallas_call(
-        functools.partial(head_kernel, rows),
-        out_shape=(whole, whole),
-        in_specs=[vmem] * 8,
-        out_specs=(vmem, vmem),
-        scratch_shapes=[
-            pltpu.VMEM((chunks, size, size), BF16),
-            pltpu.VMEM((chunks, size, size), BF16),
+    anywhere = pl.BlockSpec(memory_space=pl.ANY)
+    return pl.pallas_call(
+        functools.partial(head_kernel, devices),
+        out_shape=(slab, slab),
+        in_specs=[anywhere] * 5 + [vmem] * 2,
+        out_specs=(anywhere, anywhere),
+        scratch_shapes=[pltpu.VMEM((tokens, size), BF16)] * 5
+        + [pltpu.VMEM((devices, 4 * per, CHUNK), F32)]
+        + [pltpu.VMEM((tokens, size), BF16)] * 2
+        + [pltpu.VMEM((chunks, size, size), BF16)] * 2
+        + [
             pltpu.VMEM((tokens, size), F32),
+            pltpu.SemaphoreType.DMA((8, devices)),
+            pltpu.SemaphoreType.DMA((8, devices)),
+            pltpu.SemaphoreType.DMA((8,)),
         ],
-        compiler_params=pltpu.CompilerParams(vmem_limit_bytes=56 * 1024 * 1024),
-    )(q, k, v, mq, mk, cum, gate, ridge)
-
-    def to_slabs(a):
-        return lax.all_to_all(a, "seq", 0, 1, tiled=True)
-
-    return to_slabs(att), to_slabs(out)
+        compiler_params=pltpu.CompilerParams(
+            collective_id=0, has_side_effects=True, vmem_limit_bytes=56 * 1024 * 1024
+        ),
+    )(attn_query, attn_key, attn_value, mesa_key, mesa_query, rates, regularizer)
 
 
 def fits_heads(mesh, rows, heads, size):
@@ -428,6 +520,8 @@
         mesh.shape["seq"] == heads
         and size == CHUNK
         and WINDOW % rows == 0
+        and rows % CHUNK == 0
+        and WAYS % (rows // CHUNK) == 0
         and tokens % (CHUNK * WAYS) == 0
     )
 

time: 307 us -> 221 us (0.72)
  Pallas kernels: 79.7 us -> 214 us
  waiting for transfers between devices: 132 us -> 0 us
  starting transfers between devices: 42.8 us -> 0 us
  blocking collectives: 29.7 us -> 0 us
  local copies, waits for them, and re-layouts: 17.9 us -> 4.91 us
    pallas_call x1, Pallas kernels: 79.7 us -> 214 us  [head_body(): pl.pallas_call(functools.partial(head_kernel, devices), out_shape=(slab,...]
    all_to_all x7 -> x0, waiting for transfers between devices: 132 us -> none  [the longest x5 108 us: to_heads(): return lax.all_to_all(a, 'seq', 1, 0, tiled=True)]
    all_to_all x7 -> x0, starting transfers between devices: 42.8 us -> none  [the longest x5 30.8 us: to_heads(): return lax.all_to_all(a, 'seq', 1, 0, tiled=True)]
    all_to_all x1 -> x0, blocking collectives: 29.7 us -> none  [to_slabs(): return lax.all_to_all(a, 'seq', 0, 1, tiled=True)]
    all_to_all x7 -> x0, local copies, waits for them, and re-layouts: 12.2 us -> none  [the longest x5 9.91 us: to_heads(): return lax.all_to_all(a, 'seq', 1, 0, tiled=True)]
  transfers between devices with their start and end apart: 7 -> 0, of which waited for: 7 -> 0; matrix products, arithmetic and copies ran while one was open for 5% -> 0% of each run, Pallas kernels for 0% -> 0%
where the time goes in v2:
time: 221 us; the launch traced here: 220 us
  Pallas kernels  214 us (97%)
  local copies, waits for them, and re-layouts  4.91 us (2%)
    pallas_call x1, Pallas kernels, head_body(): pl.pallas_call(functools.partial(head_kernel, devices), out_shape=(slab,...  214 us

profile of v2, /device:TPU:29, one launch (start us, length us, event | category | flops | bytes accessed | tf_op | source)
XLA Modules:
  0.0 220.3 jit_solution(9188789628892987452)
XLA Ops:
  0.6 0.0 copy-start.1
  0.6 0.7 reshape.11
  1.4 0.0 copy-done.1
  1.4 0.1 copy.12
  1.5 0.2 reduce_window_sum.11
  1.7 0.1 copy.11
  1.8 0.6 pad.4.refs_5_
  2.4 214.5 %shard_map.95 = (bf16[256,2048]{1,0:T(8,128)(2,1)}, bf16[256,2048]{1,0:T(8,128)(2,1)}) custom-call(bf16[256,2048]{1,0:T(8,128)(2,1)} %refs_0_.1, bf16[256,2048]{1,0:T(8,128)(2,1)} %refs_1_.1, bf16[256,2048]{1,0:T(8,128)(2,1)} %refs_2_.1, bf16[256,2048]{1,0:T(8,128)(2,1)} %refs_3_.1, bf16[256,2048]{1,0:T(8,128)(2,1)} %refs_4_.1, f32[16,8,128]{2,1,0:T(8,128)} %pad.4.refs_5_, ...), custom_call_target="tpu_custom_call" | custom-call | tf_op jit(solution)/shard_map/pallas_call | solution.py:496
  216.9 0.0 copy-start
  216.9 2.4 %copy.15 = bf16[256,2048]{1,0:T(8,128)(2,1)} copy(bf16[256,2048]{1,0:T(8,128)(2,1)} %get-tuple-element.4) | data formatting | bytes 2097152
  219.3 0.0 copy-done
  219.3 1.0 copy.16
  (1 shorter events, 0.0 us)
Async XLA Ops:
  0.6 0.7 copy-start.1
  216.9 2.4 %copy-start = (bf16[256,2048]{1,0:T(8,128)(2,1)S(1)}, bf16[256,2048]{1,0:T(8,128)(2,1)}, u32[]{:S(2)}) copy-start(bf16[256,2048]{1,0:T(8,128)(2,1)} %get-tuple-element.5) | copy-start | bytes 3145732

commit v3 on v2

--- a/solution.py
+++ b/solution.py
@@ -243,29 +243,30 @@
     out_ref[pl.ds(pl.multiple_of(i * rows, rows), rows), :] = (summed / total).astype(BF16)
 
 
-def attend_all(q_ref, k_ref, v_ref, out_ref, rows, done):
+def attend_all(q_ref, k_ref, v_ref, out_ref, rows, order, done):
     blocks = q_ref.shape[0] // rows
     reach = WINDOW // rows
     early = min(reach, blocks)
-    for low in range(0, early, 2):
-        high = min(low + 2, early)
-
-        def one(i, carry, high=high):
-            attend_block(q_ref, k_ref, v_ref, out_ref, i, 0, high, rows, False)
-            done(i)
-            return carry
-
-        lax.fori_loop(low, high, one, 0)
-    if blocks > reach:
-
-        def late(i, carry):
-            attend_block(
-                q_ref, k_ref, v_ref, out_ref, i, i - reach, reach + 1, rows, True
-            )
-            done(i)
-            return carry
-
-        lax.fori_loop(reach, blocks, late, 0)
+
+    def one(t, carry):
+        i = order(t)
+        for low in range(0, early, 2):
+            high = min(low + 2, early)
+
+            @pl.when((i >= low) & (i < high))
+            def _(high=high):
+                attend_block(q_ref, k_ref, v_ref, out_ref, i, 0, high, rows, False)
+
+        if blocks > reach:
+
+            @pl.when(i >= reach)
+            def _():
+                attend_block(q_ref, k_ref, v_ref, out_ref, i, i - reach, reach + 1, rows, True)
+
+        done(i)
+        return carry
+
+    lax.fori_loop(0, blocks, one, 0)
 
 
 def flat(c, per):
@@ -454,14 +455,14 @@
         over_peers(lambda peer: remote(a, me, peer, peer).start())
         local(a).start()
 
-    for a in (0, 1, 2):
-        arrive(a)
-    attend_all(q, k, v, att, rows, lambda i: give(6, i))
     for a in (5, 3, 4):
         arrive(a)
     gram_states(mk, mk, rates, gram)
+    solve_all(mq, mk, rates, ridge_in[pl.ds(me, 1), :], gram, x)
+    for a in (0, 1, 2):
+        arrive(a)
+    attend_all(q, k, v, att, rows, lambda t: other(t + 1), lambda i: give(6, i))
     gram_states(mk, att, rates, cross)
-    solve_all(mq, mk, rates, ridge_in[pl.ds(me, 1), :], gram, x)
 
     def slab_out(t, carry):
         slab = other(t + 1)
@@ -476,7 +477,7 @@
         over_peers(lambda peer: remote(a, me, peer, peer).wait_send())
 
 
-SEND_ORDER = (0, 1, 2, 5, 3, 4)
+SEND_ORDER = (5, 3, 4, 0, 1, 2)
 
 
 def head_body(

time: 221 us -> 181 us (0.82)
  Pallas kernels: 214 us -> 175 us
    pallas_call x1, Pallas kernels: 214 us -> 175 us  [head_body(): pl.pallas_call(functools.partial(head_kernel, devices), out_shape=(slab,...]
where the time goes in v3:
time: 181 us; the launch traced here: 180 us
  Pallas kernels  175 us (97%)
  local copies, waits for them, and re-layouts  4.91 us (3%)
    pallas_call x1, Pallas kernels, head_body(): pl.pallas_call(functools.partial(head_kernel, devices), out_shape=(slab,...  175 us

profile of v3, /device:TPU:29, one launch (start us, length us, event | category | flops | bytes accessed | tf_op | source)
XLA Modules:
  0.0 180.4 jit_solution(4610393513713693110)
XLA Ops:
  0.6 0.0 copy-start.1
  0.6 0.7 reshape.11
  1.4 0.0 copy-done.1
  1.4 0.1 copy.12
  1.5 0.2 reduce_window_sum.11
  1.7 0.1 copy.11
  1.8 0.6 pad.4.refs_5_
  2.4 174.6 %shard_map.95 = (bf16[256,2048]{1,0:T(8,128)(2,1)}, bf16[256,2048]{1,0:T(8,128)(2,1)}) custom-call(bf16[256,2048]{1,0:T(8,128)(2,1)} %refs_0_.1, bf16[256,2048]{1,0:T(8,128)(2,1)} %refs_1_.1, bf16[256,2048]{1,0:T(8,128)(2,1)} %refs_2_.1, bf16[256,2048]{1,0:T(8,128)(2,1)} %refs_3_.1, bf16[256,2048]{1,0:T(8,128)(2,1)} %refs_4_.1, f32[16,8,128]{2,1,0:T(8,128)} %pad.4.refs_5_, ...), custom_call_target="tpu_custom_call" | custom-call | tf_op jit(solution)/shard_map/pallas_call | solution.py:497
  177.0 0.0 copy-start
  177.0 2.4 %copy.15 = bf16[256,2048]{1,0:T(8,128)(2,1)} copy(bf16[256,2048]{1,0:T(8,128)(2,1)} %get-tuple-element.4) | data formatting | bytes 2097152
  179.4 0.0 copy-done
  179.4 1.0 copy.16
  (1 shorter events, 0.0 us)
Async XLA Ops:
  0.6 0.7 copy-start.1
  177.0 2.4 %copy-start = (bf16[256,2048]{1,0:T(8,128)(2,1)S(1)}, bf16[256,2048]{1,0:T(8,128)(2,1)}, u32[]{:S(2)}) copy-start(bf16[256,2048]{1,0:T(8,128)(2,1)} %get-tuple-element.5) | copy-start | bytes 3145732

commit v4 on v3

--- a/solution.py
+++ b/solution.py
@@ -363,8 +363,12 @@
             return tuple(out)
 
         state = lax.fori_loop(0, CG_ITERS, sweep, tuple(state))
-        for c, s in zip(ids, state):
-            x_ref[span(c, per), :] = s[0]
+        for w, (c, s) in enumerate(zip(ids, state)):
+            mix, start = mixes[w]
+            products = dot(two_terms(s[0]), jnp.concatenate([keys[w]] * 2, axis=1), NT)
+            x_ref[span(c, per), :] = jnp.concatenate(
+                [two_terms(start * s[0]), two_terms(mix * products)], axis=1
+            )
         return carry
 
     lax.fori_loop(0, chunks // WAYS, group, 0)
@@ -373,12 +377,10 @@
 def read_out(k_ref, v_ref, rates_ref, cross_ref, x_ref, out_ref, slab):
     per = rates_ref.shape[1] // 4
     for c in chunk_ids(slab, per, per):
-        mix, start = mix_of(rates_ref, c)
-        keys, values, cross = k_ref[span(c, per), :], v_ref[span(c, per), :], cross_ref[flat(c, per)]
-        x = two_terms(x_ref[span(c, per), :])
-        products = dot(x, jnp.concatenate([keys, keys], axis=1), NT)
-        rows = start * dot(x, jnp.concatenate([cross, cross], axis=0))
-        rows = rows + dot(two_terms(mix * products), jnp.concatenate([values, values], axis=0))
+        values, cross = v_ref[span(c, per), :], cross_ref[flat(c, per)]
+        rows = dot(
+            x_ref[span(c, per), :], jnp.concatenate([cross, cross, values, values], axis=0)
+        )
         out_ref[span(c, per), :] = rows.astype(BF16)
 
 
@@ -504,7 +506,7 @@
         + [pltpu.VMEM((tokens, size), BF16)] * 2
         + [pltpu.VMEM((chunks, size, size), BF16)] * 2
         + [
-            pltpu.VMEM((tokens, size), F32),
+            pltpu.VMEM((tokens, 4 * size), BF16),
             pltpu.SemaphoreType.DMA((8, devices)),
             pltpu.SemaphoreType.DMA((8, devices)),
             pltpu.SemaphoreType.DMA((8,)),

time: 181 us -> 182 us (level)
  no operation moved by 1% of the time
where the time goes in v4:
time: 182 us
  Pallas kernels  176 us (97%)
  local copies, waits for them, and re-layouts  4.91 us (3%)
    pallas_call x1, Pallas kernels, head_body(): pl.pallas_call(functools.partial(head_kernel, devices), out_shape=(slab,...  176 us

profile of v4, /device:TPU:29, one launch (start us, length us, event | category | flops | bytes accessed | tf_op | source)
XLA Modules:
  0.0 181.6 jit_solution(13683610992157951474)
XLA Ops:
  0.6 0.0 copy-start.1
  0.6 0.7 reshape.11
  1.4 0.0 copy-done.1
  1.4 0.1 copy.12
  1.5 0.2 reduce_window_sum.11
  1.7 0.1 copy.11
  1.8 0.6 pad.4.refs_5_
  2.4 175.8 %shard_map.95 = (bf16[256,2048]{1,0:T(8,128)(2,1)}, bf16[256,2048]{1,0:T(8,128)(2,1)}) custom-call(bf16[256,2048]{1,0:T(8,128)(2,1)} %refs_0_.1, bf16[256,2048]{1,0:T(8,128)(2,1)} %refs_1_.1, bf16[256,2048]{1,0:T(8,128)(2,1)} %refs_2_.1, bf16[256,2048]{1,0:T(8,128)(2,1)} %refs_3_.1, bf16[256,2048]{1,0:T(8,128)(2,1)} %refs_4_.1, f32[16,8,128]{2,1,0:T(8,128)} %pad.4.refs_5_, ...), custom_call_target="tpu_custom_call" | custom-call | tf_op jit(solution)/shard_map/pallas_call | solution.py:499
  178.2 0.0 copy-start
  178.2 2.4 %copy.15 = bf16[256,2048]{1,0:T(8,128)(2,1)} copy(bf16[256,2048]{1,0:T(8,128)(2,1)} %get-tuple-element.4) | data formatting | bytes 2097152
  180.6 0.0 copy-done
  180.6 1.0 copy.16
  (1 shorter events, 0.0 us)
Async XLA Ops:
  0.6 0.7 copy-start.1
  178.2 2.4 %copy-start = (bf16[256,2048]{1,0:T(8,128)(2,1)S(1)}, bf16[256,2048]{1,0:T(8,128)(2,1)}, u32[]{:S(2)}) copy-start(bf16[256,2048]{1,0:T(8,128)(2,1)} %get-tuple-element.5) | copy-start | bytes 3145732
